TPU v7x, 32 devices: a whole 2x2x4 slice. The times are simulated.
32 devices in a mesh: grp: 4 (over y, x), dev: 8 (over z, core).
Axes of the slice: x: 2, y: 2, z: 4, core: 2. Of those that a mesh axis runs over, the one named last changes fastest.
Arguments:
- points: bfloat16 [65536, 256], P(('grp', 'dev')), may hold values from -6 to 6
- ridge: float32 [1024], replicated, may hold values from 0.25 to 2
- landmark_ids: int32 [1024], replicated, may hold values from 0 to 65535, as said below
Outputs:
- features: bfloat16 [65536, 1024], P(('grp', 'dev'))
Inputs may be any that keep to these rules, and one draw needn't show every extreme that they name: `landmark_ids`: sorted ascending, all distinct.
All inputs are finite; a program needn't handle non-finite values.
Results may differ from a plain program's by a relative error of at most 0.0015.
Values may be sent and summed in bfloat16 or wider, within the bound.
No kernel may reach another device: no remote copies, remote signals or barrier semaphores. Data moves between devices by JAX's collectives and lax.ppermute only.
A program may use at most 128 MiB of HBM per device.

v0:
```python
import jax
import jax.numpy as jnp
from jax import lax
from jax.sharding import PartitionSpec as P


def kernel_block(left, right):
    left_sq = jnp.sum(jnp.square(left.astype(jnp.float32)), axis=1)
    right_sq = jnp.sum(jnp.square(right.astype(jnp.float32)), axis=1)
    inner = jnp.dot(left, right.T, preferred_element_type=jnp.float32)
    width = left.shape[1]
    return jnp.exp(-(left_sq[:, None] + right_sq[None, :] - 2.0 * inner) / (2.0 * width))


def shards(points, ridge, landmark_ids):
    count = points.shape[0]
    start = lax.axis_index(("grp", "dev")) * count
    offset = landmark_ids - start
    inside = (offset >= 0) & (offset < count)
    picked = points[jnp.clip(offset, 0, count - 1)]
    filled = jnp.where(inside[:, None], picked.astype(jnp.float32), 0.0)
    marks = lax.psum(filled, ("grp", "dev")).astype(jnp.bfloat16)
    core = kernel_block(marks, marks) + jnp.diag(ridge)
    lower = jnp.linalg.cholesky(core)
    cross = kernel_block(points, marks)
    raw = lax.linalg.triangular_solve(lower, cross, left_side=False, lower=True, transpose_a=True)
    total_rows = count * lax.axis_size(("grp", "dev"))
    totals, squares = lax.psum(
        (jnp.sum(raw, axis=0), jnp.sum(jnp.square(raw), axis=0)), ("grp", "dev")
    )
    mean = totals / total_rows
    var = jnp.maximum(squares / total_rows - jnp.square(mean), 0.0)
    centered = raw - mean[None, :]
    return (centered / jnp.sqrt(var + 1e-05)[None, :]).astype(jnp.bfloat16)


def solution(mesh):
    placed = (P(("grp", "dev"), None), P(), P())
    return jax.shard_map(
        shards, mesh=mesh, in_specs=placed, out_specs=P(("grp", "dev"), None), check_vma=False
    )
```

profile of v0, /device:TPU:0, one launch (start us, length us, event | category | flops | bytes accessed | tf_op | source)
XLA Modules:
  0.0 495.3 jit_solution(2860757767389505931)
XLA Ops:
  8.1 53.3 %all-reduce.3 = bf16[1024,256]{1,0:T(8,128)(2,1)S(1)} all-reduce(f32[1024,256]{1,0:T(8,128)S(1)} %convert_select_fusion), channel_id=1, replica_groups=mesh['grp'=4,'dev'=8] {'grp','dev'}, use_global_device_ids=true, to_apply=%region_1.2 | all-reduce | flops 262144 | bytes 1572864 | tf_op jit(solution)/shard_map/psum | solution.py:22
  66.0 5.6 %subtract_negate_fusion = (f32[1024,1024]{0,1:T(8,128)}, f32[1024,1024]{0,1:T(8,128)}, f32[1024,1024]{0,1:T(8,128)}) fusion(f32[1024]{0:T(1024)S(1)} %multiply_reduce_fusion.2, bf16[1024,256]{1,0:T(8,128)(2,1)S(1)} %all-reduce.3), kind=kOutput, calls=%fused_computation.27 | convolution fusion | flops 541065216 | bytes 13111296 | tf_op jit(solution)/shard_map/dot_general | solution.py:10
  71.6 5.4 %copy.5 = f32[1024,1024]{1,0:T(8,128)} copy(f32[1024,1024]{0,1:T(8,128)} %get-tuple-element.76) | data formatting | bytes 8388608 | tf_op jit(solution)/shard_map/neg | solution.py:12
  82.3 6.3 %fusion.16 = f32[1024,1024]{1,0:T(8,128)S(1)} fusion(f32[1024,1024]{1,0:T(8,128)} %copy.6, f32[1024,1024]{1,0:T(8,128)} %copy.5, f32[1024,1024]{0,1:T(8,128)} %get-tuple-element.78, f32[1024]{0:T(1024)S(1)} %copy-done.5), kind=kLoop, calls=%fused_computation.24 | loop fusion | flops 13631488 | bytes 16781312 | tf_op jit(solution)/shard_map/jit(cholesky)/div | solution.py:24
  90.6 11.7 %cholesky.222 = f32[128,128]{1,0:T(8,128)S(1)} custom-call(f32[128,128]{1,0:T(8,128)S(1)} %cholesky.577), custom_call_target="Cholesky" | custom-call | tf_op jit(solution)/shard_map/jit(cholesky)/cholesky | solution.py:24
  102.4 9.8 %custom-call.62 = f32[1,128,128]{1,2,0:T(8,128)S(1)} custom-call(f32[1,128,128]{2,1,0:T(8,128)S(1)} %get-tuple-element.73), custom_call_target="InvertDiagBlocksLowerTriangular" | custom-call | tf_op jit(solution)/shard_map/jit(cholesky)/cholesky | solution.py:24
  118.6 11.7 %cholesky.243 = f32[128,128]{1,0:T(8,128)S(1)} custom-call(f32[128,128]{1,0:T(8,128)S(1)} %cholesky.581), custom_call_target="Cholesky" | custom-call | tf_op jit(solution)/shard_map/jit(cholesky)/cholesky | solution.py:24
  132.9 10.2 %custom-call.63 = f32[1,128,128]{1,2,0:T(8,128)S(1)} custom-call(f32[1,128,128]{2,1,0:T(8,128)S(1)} %get-tuple-element.70), custom_call_target="InvertDiagBlocksLowerTriangular" | custom-call | tf_op jit(solution)/shard_map/jit(cholesky)/cholesky | solution.py:24
  146.4 11.7 %cholesky.466 = f32[128,128]{1,0:T(8,128)S(1)} custom-call(f32[128,128]{1,0:T(8,128)S(1)} %cholesky.586), custom_call_target="Cholesky" | custom-call | tf_op jit(solution)/shard_map/jit(cholesky)/cholesky | solution.py:24
  160.1 9.8 %custom-call.64 = f32[1,128,128]{1,2,0:T(8,128)S(1)} custom-call(f32[1,128,128]{2,1,0:T(8,128)S(1)} %get-tuple-element.67), custom_call_target="InvertDiagBlocksLowerTriangular" | custom-call | tf_op jit(solution)/shard_map/jit(cholesky)/cholesky | solution.py:24
  173.4 11.9 %cholesky.485 = f32[128,128]{1,0:T(8,128)S(1)} custom-call(f32[128,128]{1,0:T(8,128)S(1)} %cholesky.591), custom_call_target="Cholesky" | custom-call | tf_op jit(solution)/shard_map/jit(cholesky)/cholesky | solution.py:24
  187.2 9.8 %custom-call.65 = f32[1,128,128]{1,2,0:T(8,128)S(1)} custom-call(f32[1,128,128]{2,1,0:T(8,128)S(1)} %get-tuple-element.64), custom_call_target="InvertDiagBlocksLowerTriangular" | custom-call | tf_op jit(solution)/shard_map/jit(cholesky)/cholesky | solution.py:24
  200.4 11.7 %cholesky.504 = f32[128,128]{1,0:T(8,128)S(1)} custom-call(f32[128,128]{1,0:T(8,128)S(1)} %cholesky.596), custom_call_target="Cholesky" | custom-call | tf_op jit(solution)/shard_map/jit(cholesky)/cholesky | solution.py:24
  214.0 9.8 %custom-call.66 = f32[1,128,128]{1,2,0:T(8,128)S(1)} custom-call(f32[1,128,128]{2,1,0:T(8,128)S(1)} %get-tuple-element.61), custom_call_target="InvertDiagBlocksLowerTriangular" | custom-call | tf_op jit(solution)/shard_map/jit(cholesky)/cholesky | solution.py:24
  227.4 11.7 %cholesky.524 = f32[128,128]{1,0:T(8,128)S(1)} custom-call(f32[128,128]{1,0:T(8,128)S(1)} %cholesky.601), custom_call_target="Cholesky" | custom-call | tf_op jit(solution)/shard_map/jit(cholesky)/cholesky | solution.py:24
  241.0 9.8 %custom-call.67 = f32[1,128,128]{1,2,0:T(8,128)S(1)} custom-call(f32[1,128,128]{2,1,0:T(8,128)S(1)} %get-tuple-element.58), custom_call_target="InvertDiagBlocksLowerTriangular" | custom-call | tf_op jit(solution)/shard_map/jit(cholesky)/cholesky | solution.py:24
  253.9 11.7 %cholesky.544 = f32[128,128]{1,0:T(8,128)S(1)} custom-call(f32[128,128]{1,0:T(8,128)S(1)} %cholesky.606), custom_call_target="Cholesky" | custom-call | tf_op jit(solution)/shard_map/jit(cholesky)/cholesky | solution.py:24
  267.5 10.2 %custom-call.68 = f32[1,128,128]{1,2,0:T(8,128)S(1)} custom-call(f32[1,128,128]{2,1,0:T(8,128)S(1)} %get-tuple-element.55), custom_call_target="InvertDiagBlocksLowerTriangular" | custom-call | tf_op jit(solution)/shard_map/jit(cholesky)/cholesky | solution.py:24
  280.4 11.7 %cholesky.562 = f32[128,128]{1,0:T(8,128)S(1)} custom-call(f32[128,128]{1,0:T(8,128)S(1)} %convolution_subtract_fusion.11), custom_call_target="Cholesky" | custom-call | tf_op jit(solution)/shard_map/jit(cholesky)/cholesky | solution.py:24
  298.8 22.5 %while.1 = (s32[]{:T(128)}, f32[1024,1024]{1,0:T(8,128)}, s32[8,2]{0,1:T(2,128)S(1)}, f32[8,128,128]{2,1,0:T(8,128)S(1)}, s32[]{:T(128)}) while((s32[]{:T(128)}, f32[1024,1024]{1,0:T(8,128)}, s32[8,2]{0,1:T(2,128)S(1)}, f32[8,128,128]{2,1,0:T(8,128)S(1)}, s32[]{:T(128)}) %tuple.61), condition=%wide.while_cond, body=%wide.while_body.sunk | while | flops 2 | bytes 131189 | solution.py:26
  321.2 78.8 %custom-call.69 = f32[8,128,128]{1,2,0:T(8,128)S(1)} custom-call(f32[8,128,128]{2,1,0:T(8,128)S(1)} %get-tuple-element.12), custom_call_target="InvertDiagBlocksLowerTriangular" | custom-call | tf_op jit(solution)/shard_map/triangular_solve | solution.py:26
  434.2 5.8 %convolution_subtract_fusion.1 = f32[2048,128]{0,1:T(8,128)S(1)} fusion(f32[2048,896]{0,1:T(8,128)S(1)} %get-tuple-element.27, f32[2048,1024]{0,1:T(8,128)S(1)} %bitcast.124, f32[1024,1024]{1,0:T(8,128)} %get-tuple-element.131), kind=kOutput, calls=%fused_computation.38 | convolution fusion | flops 2818834432 | bytes 9895936 | tf_op jit(solution)/shard_map/triangular_solve | solution.py:26
  444.3 38.9 %all-reduce.1 = (f32[1024]{0:T(1024)S(1)}, f32[1024]{0:T(1024)S(1)}) all-reduce(f32[1024]{0:T(1024)S(1)} %get-tuple-element.14, f32[1024]{0:T(1024)S(1)} %get-tuple-element.13), channel_id=1, replica_groups=mesh['grp'=4,'dev'=8] {'grp','dev'}, use_global_device_ids=true, to_apply=%region_22.23 | all-reduce | flops 2048 | bytes 16384 | tf_op jit(solution)/shard_map/psum | solution.py:28
  488.5 6.4 %copy.7 = bf16[2048,1024]{1,0:T(8,128)(2,1)} copy(bf16[2048,1024]{0,1:T(8,128)(2,1)} %divide_convert_fusion) | data formatting | bytes 8388608 | tf_op jit(solution)/shard_map/convert_element_type | solution.py:34
  (107 shorter events, 125.8 us)
Async XLA Ops:
  3.0 58.6 %copy-start.1 = (bf16[2048,256]{1,0:T(8,128)(2,1)S(1)}, bf16[2048,256]{1,0:T(8,128)(2,1)}, u32[]{:S(2)}) copy-start(bf16[2048,256]{1,0:T(8,128)(2,1)} %param.3) | copy-start | bytes 3145732
  76.9 5.4 %copy-start.5 = (f32[1024]{0:T(1024)S(1)}, f32[1024]{0:T(1024)}, u32[]{:S(2)}) copy-start(f32[1024]{0:T(1024)} %param.4) | copy-start | bytes 12292
  88.6 2.0 copy-start.2
  400.0 5.3 %copy-start.3 = (f32[8,128,128]{1,2,0:T(8,128)}, f32[8,128,128]{1,2,0:T(8,128)S(1)}, u32[]{:S(2)}) copy-start(f32[8,128,128]{1,2,0:T(8,128)S(1)} %custom-call.69) | copy-start | bytes 1572868
  400.0 6.6 %slice-start = ((s8[8388608]{0:T(1024)(128)(4,1)}), s8[4194304]{0:T(1024)(128)(4,1)S(1)}, s32[]{:S(2)}) async-start(s8[8388608]{0:T(1024)(128)(4,1)} %bitcast.123), calls=%async_computation | async-start | bytes 8388608
  402.8 3.8 slice-start.1
  406.6 2.3 copy-start.4
  441.0 3.2 copy-start
where the time goes:
time: 502 us; the launch traced here: 495 us
  other arithmetic  272 us (54%)
  blocking collectives  92.1 us (18%)
  matrix products  74 us (15%)
  local copies, waits for them, and re-layouts  51 us (10%)
  between operations  5.8 us (1%)
    another operation x30, other arithmetic, shards(): lower = jnp.linalg.cholesky(core)  172 us
    another operation x3, other arithmetic, shards(): lax.linalg.triangular_solve(lower, cross, left_side=False, lower=True, tr...  83.7 us
    psum x1, blocking collectives, shards(): marks = lax.psum(filled, ('grp', 'dev')).astype(jnp.bfloat16)  53.3 us
    another operation x15, matrix products, shards(): lax.linalg.triangular_solve(lower, cross, left_side=False, lower=True, tr...  40.8 us
    psum x1, blocking collectives, shards(): lax.psum((jnp.sum(raw, axis=0), jnp.sum(jnp.square(raw), axis=0)), ('grp'...  38.9 us
    another operation x14, matrix products, shards(): lower = jnp.linalg.cholesky(core)  23.2 us
    another operation x24, local copies, waits for them, and re-layouts  22.3 us

commit v1 on v0

--- a/solution.py
+++ b/solution.py
@@ -2,6 +2,7 @@
 import jax.numpy as jnp
 from jax import lax
 from jax.sharding import PartitionSpec as P
+from jax.lax import all_gather
 
 
 def kernel_block(left, right):
@@ -13,13 +14,17 @@
 
 
 def shards(points, ridge, landmark_ids):
+
+    def solve_windows(mat):
+        return all_gather(mat, axis_name=("grp", "dev")).sum(axis=0)
+
     count = points.shape[0]
     start = lax.axis_index(("grp", "dev")) * count
     offset = landmark_ids - start
     inside = (offset >= 0) & (offset < count)
     picked = points[jnp.clip(offset, 0, count - 1)]
     filled = jnp.where(inside[:, None], picked.astype(jnp.float32), 0.0)
-    marks = lax.psum(filled, ("grp", "dev")).astype(jnp.bfloat16)
+    marks = solve_windows(filled).astype(jnp.bfloat16)
     core = kernel_block(marks, marks) + jnp.diag(ridge)
     lower = jnp.linalg.cholesky(core)
     cross = kernel_block(points, marks)

time: 502 us -> 672 us (1.34)
  waiting for transfers between devices: 0 us -> 197 us
  blocking collectives: 92.1 us -> 38.4 us
  between operations: 5.8 us -> 19 us
  other arithmetic: 272 us -> 284 us
    all_gather x0 -> x1, waiting for transfers between devices: none -> 197 us  [solve_windows(): return all_gather(mat, axis_name=('grp', 'dev')).sum(axis=0)]
    psum x1 -> x0, blocking collectives: 53.3 us -> none  [shards(): marks = lax.psum(filled, ('grp', 'dev')).astype(jnp.bfloat16)]
    reduce_sum x0 -> x1, other arithmetic: none -> 12 us  [solve_windows(): return all_gather(mat, axis_name=('grp', 'dev')).sum(axis=0)]
  transfers between devices with their start and end apart: 0 -> 1, of which waited for: 0 -> 1; matrix products, arithmetic and copies ran while one was open for 0% -> 0% of each run, Pallas kernels for 0% -> 0%
where the time goes in v1:
time: 672 us; the launch traced here: 663 us
  other arithmetic  284 us (42%)
  waiting for transfers between devices  197 us (29%)
  matrix products  74.6 us (11%)
  local copies, waits for them, and re-layouts  50.9 us (8%)
  blocking collectives  38.4 us (6%)
  between operations  19 us (3%)
    all_gather x1, waiting for transfers between devices, solve_windows(): return all_gather(mat, axis_name=('grp', 'dev')).sum(axis=0)  197 us
    another operation x30, other arithmetic, shards(): lower = jnp.linalg.cholesky(core)  172 us
    another operation x3, other arithmetic, shards(): lax.linalg.triangular_solve(lower, cross, left_side=False, lower=True, tr...  83.5 us
    another operation x15, matrix products, shards(): lax.linalg.triangular_solve(lower, cross, left_side=False, lower=True, tr...  41 us
    psum x1, blocking collectives, shards(): lax.psum((jnp.sum(raw, axis=0), jnp.sum(jnp.square(raw), axis=0)), ('grp'...  38.4 us
    another operation x14, matrix products, shards(): lower = jnp.linalg.cholesky(core)  23.3 us
    another operation x24, local copies, waits for them, and re-layouts  22.3 us
  transfers between devices with their start and end apart: 1, of which 1 were waited for; matrix products, arithmetic and copies ran while one was open for 0% of the time, Pallas kernels for 0%

profile of v1, /device:TPU:0, one launch (start us, length us, event | category | flops | bytes accessed | tf_op | source)
XLA Modules:
  0.0 663.3 jit_solution(14990910626862469653)
XLA Ops:
  14.4 196.7 %all-gather.2.cloned.1.call-done = f32[32,1024,256]{2,1,0:T(8,128)} async-done(((f32[1,1024,256]{2,1,0:T(8,128)}), f32[32,1024,256]{2,1,0:T(8,128)}) %all-gather.2.cloned.1.call-update) | async-done | bytes 33554448 | tf_op jit(solution)/shard_map/all_gather | solution.py:19
  211.1 12.0 %reduce_sum.44 = bf16[1024,256]{1,0:T(8,128)(2,1)S(1)} reduce(f32[32,1024,256]{2,1,0:T(8,128)} %all-gather.2.cloned.1.call-done, f32[]{:T(128)} %constant.289.clone.1), dimensions={0}, to_apply=%region_1.2 | reduce | flops 8126464 | bytes 34078724 | tf_op jit(solution)/shard_map/reduce_sum | solution.py:19
  223.3 5.6 subtract_negate_fusion
  239.6 6.1 fusion.16
  247.7 11.7 %cholesky.222 = f32[128,128]{1,0:T(8,128)S(1)} custom-call(f32[128,128]{1,0:T(8,128)S(1)} %cholesky.577), custom_call_target="Cholesky" | custom-call | tf_op jit(solution)/shard_map/jit(cholesky)/cholesky | solution.py:29
  266.8 9.8 %custom-call.62 = f32[1,128,128]{1,2,0:T(8,128)S(1)} custom-call(f32[1,128,128]{2,1,0:T(8,128)S(1)} %get-tuple-element.73), custom_call_target="InvertDiagBlocksLowerTriangular" | custom-call | tf_op jit(solution)/shard_map/jit(cholesky)/cholesky | solution.py:29
  280.5 11.7 %cholesky.243 = f32[128,128]{1,0:T(8,128)S(1)} custom-call(f32[128,128]{1,0:T(8,128)S(1)} %cholesky.581), custom_call_target="Cholesky" | custom-call | tf_op jit(solution)/shard_map/jit(cholesky)/cholesky | solution.py:29
  292.8 9.8 %custom-call.63 = f32[1,128,128]{1,2,0:T(8,128)S(1)} custom-call(f32[1,128,128]{2,1,0:T(8,128)S(1)} %get-tuple-element.70), custom_call_target="InvertDiagBlocksLowerTriangular" | custom-call | tf_op jit(solution)/shard_map/jit(cholesky)/cholesky | solution.py:29
  305.9 11.9 %cholesky.466 = f32[128,128]{1,0:T(8,128)S(1)} custom-call(f32[128,128]{1,0:T(8,128)S(1)} %cholesky.586), custom_call_target="Cholesky" | custom-call | tf_op jit(solution)/shard_map/jit(cholesky)/cholesky | solution.py:29
  319.1 9.8 %custom-call.64 = f32[1,128,128]{1,2,0:T(8,128)S(1)} custom-call(f32[1,128,128]{2,1,0:T(8,128)S(1)} %get-tuple-element.67), custom_call_target="InvertDiagBlocksLowerTriangular" | custom-call | tf_op jit(solution)/shard_map/jit(cholesky)/cholesky | solution.py:29
  332.4 11.7 %cholesky.485 = f32[128,128]{1,0:T(8,128)S(1)} custom-call(f32[128,128]{1,0:T(8,128)S(1)} %cholesky.591), custom_call_target="Cholesky" | custom-call | tf_op jit(solution)/shard_map/jit(cholesky)/cholesky | solution.py:29
  345.5 9.8 %custom-call.65 = f32[1,128,128]{1,2,0:T(8,128)S(1)} custom-call(f32[1,128,128]{2,1,0:T(8,128)S(1)} %get-tuple-element.64), custom_call_target="InvertDiagBlocksLowerTriangular" | custom-call | tf_op jit(solution)/shard_map/jit(cholesky)/cholesky | solution.py:29
  358.9 11.7 %cholesky.504 = f32[128,128]{1,0:T(8,128)S(1)} custom-call(f32[128,128]{1,0:T(8,128)S(1)} %cholesky.596), custom_call_target="Cholesky" | custom-call | tf_op jit(solution)/shard_map/jit(cholesky)/cholesky | solution.py:29
  372.0 9.8 %custom-call.66 = f32[1,128,128]{1,2,0:T(8,128)S(1)} custom-call(f32[1,128,128]{2,1,0:T(8,128)S(1)} %get-tuple-element.61), custom_call_target="InvertDiagBlocksLowerTriangular" | custom-call | tf_op jit(solution)/shard_map/jit(cholesky)/cholesky | solution.py:29
  385.1 12.1 %cholesky.524 = f32[128,128]{1,0:T(8,128)S(1)} custom-call(f32[128,128]{1,0:T(8,128)S(1)} %cholesky.601), custom_call_target="Cholesky" | custom-call | tf_op jit(solution)/shard_map/jit(cholesky)/cholesky | solution.py:29
  398.6 9.8 %custom-call.67 = f32[1,128,128]{1,2,0:T(8,128)S(1)} custom-call(f32[1,128,128]{2,1,0:T(8,128)S(1)} %get-tuple-element.58), custom_call_target="InvertDiagBlocksLowerTriangular" | custom-call | tf_op jit(solution)/shard_map/jit(cholesky)/cholesky | solution.py:29
  411.5 11.7 %cholesky.544 = f32[128,128]{1,0:T(8,128)S(1)} custom-call(f32[128,128]{1,0:T(8,128)S(1)} %cholesky.606), custom_call_target="Cholesky" | custom-call | tf_op jit(solution)/shard_map/jit(cholesky)/cholesky | solution.py:29
  424.6 9.8 %custom-call.68 = f32[1,128,128]{1,2,0:T(8,128)S(1)} custom-call(f32[1,128,128]{2,1,0:T(8,128)S(1)} %get-tuple-element.55), custom_call_target="InvertDiagBlocksLowerTriangular" | custom-call | tf_op jit(solution)/shard_map/jit(cholesky)/cholesky | solution.py:29
  437.0 11.9 %cholesky.562 = f32[128,128]{1,0:T(8,128)S(1)} custom-call(f32[128,128]{1,0:T(8,128)S(1)} %convolution_subtract_fusion.11), custom_call_target="Cholesky" | custom-call | tf_op jit(solution)/shard_map/jit(cholesky)/cholesky | solution.py:29
  460.6 22.5 %while.1 = (s32[]{:T(128)}, f32[1024,1024]{1,0:T(8,128)}, s32[8,2]{0,1:T(2,128)S(1)}, f32[8,128,128]{2,1,0:T(8,128)S(1)}, s32[]{:T(128)}) while((s32[]{:T(128)}, f32[1024,1024]{1,0:T(8,128)}, s32[8,2]{0,1:T(2,128)S(1)}, f32[8,128,128]{2,1,0:T(8,128)S(1)}, s32[]{:T(128)}) %tuple.61), condition=%wide.while_cond, body=%wide.while_body.sunk | while | flops 2 | bytes 131189 | solution.py:31
  483.1 78.6 %custom-call.69 = f32[8,128,128]{1,2,0:T(8,128)S(1)} custom-call(f32[8,128,128]{2,1,0:T(8,128)S(1)} %get-tuple-element.12), custom_call_target="InvertDiagBlocksLowerTriangular" | custom-call | tf_op jit(solution)/shard_map/triangular_solve | solution.py:31
  596.1 5.7 convolution_subtract_fusion.1
  606.1 38.4 %all-reduce.1 = (f32[1024]{0:T(1024)S(1)}, f32[1024]{0:T(1024)S(1)}) all-reduce(f32[1024]{0:T(1024)S(1)} %get-tuple-element.14, f32[1024]{0:T(1024)S(1)} %get-tuple-element.13), channel_id=1, replica_groups=mesh['grp'=4,'dev'=8] {'grp','dev'}, use_global_device_ids=true, to_apply=%region_22.23 | all-reduce | flops 2048 | bytes 16384 | tf_op jit(solution)/shard_map/psum | solution.py:33
  649.9 6.4 copy.22
  (110 shorter events, 131.6 us)
Async XLA Ops:
  6.5 7.5 %copy-start.1 = (bf16[2048,256]{1,0:T(8,128)(2,1)S(1)}, bf16[2048,256]{1,0:T(8,128)(2,1)}, u32[]{:S(2)}) copy-start(bf16[2048,256]{1,0:T(8,128)(2,1)} %param.3) | copy-start | bytes 3145732
  6.5 204.6 %all-gather.2.cloned.1.call-start = ((), (), s32[]{:S(2)}) async-start(), calls=%async_computation | async-start | bytes 34603008 | tf_op jit(solution)/shard_map/all_gather | solution.py:19
  234.3 5.4 copy-start.5
  245.7 2.0 copy-start.2
  561.7 5.3 copy-start.3
  561.7 6.6 slice-start
  564.5 3.8 slice-start.1
  568.3 2.3 copy-start.4
  602.9 3.2 copy-start
Sparse Core Ops, SparseCore 0:
  14.2 196.8 all-gather.1
